TPU v7x, 32 devices: a whole 2x2x4 slice. The times are simulated.
32 devices in a mesh: grp: 8 (over y, x, core), col: 4 (over z).
Axes of the slice: x: 2, y: 2, z: 4, core: 2. Of those that a mesh axis runs over, the one named last changes fastest.
Arguments:
- old_tables: bfloat16 [32, 128, 32768], P(('grp', 'col')), may hold values from -3 to 3
- table_rows: int32 [32], replicated, may hold values from 4096 to 32768, as said below
- old_plan: int32 [32], replicated, may hold values from 0 to 31, each once
- new_plan: int32 [32], replicated, may hold values from 0 to 31, each once
- ids: int32 [256, 32, 16], P(('grp', 'col')), may hold values from 0 to 32767, as said below
- bag_len: int32 [256, 32], P(('grp', 'col')), may hold values from 1 to 16
Outputs:
- new_tables: bfloat16 [32, 128, 32768], P('grp', 'col')
- pooled: float32 [256, 32, 128], P(('grp', 'col'))
Inputs may be any that keep to these rules, and one draw needn't show every extreme that they name: table_rows[t] is a multiple of 4096, and some table has exactly 32768 rows. `ids`: every id of table t lies below table_rows[t].
All inputs are finite; a program needn't handle non-finite values.
Results may differ from a plain program's by a relative error of at most 0.001.
Values may be sent and summed in bfloat16 or wider, within the bound.
A program may use at most 128 MiB of HBM per device.

v0:
```python
import jax
import jax.numpy as jnp
from jax import lax
from jax.sharding import PartitionSpec as P


def invert(permutation):
    entries = permutation.shape[0]
    across = lax.broadcasted_iota(jnp.int32, (entries, entries), 1)
    down = lax.broadcasted_iota(jnp.int32, (entries, entries), 0)
    return jnp.sum(jnp.where(permutation[None, :] == down, across, 0), axis=1)


def pool_rows(table_cols, marked):
    columns = table_cols.shape[0]
    safe_ids = jnp.maximum(marked, 0).reshape(-1)
    weights = (marked >= 0).astype(jnp.float32)
    picked = (
        jnp.take(table_cols, safe_ids, axis=1)
        .reshape(columns, marked.shape[0], marked.shape[1])
        .astype(jnp.float32)
    )
    return jnp.sum(picked * weights[None, :, :], axis=2)


def reorder_blocks(spread, source_rows):
    count = spread.shape[0]
    across = lax.broadcasted_iota(jnp.int32, (count, count), 1)
    selector = (source_rows[:, None] == across).astype(spread.dtype)
    flat = spread.reshape(count, -1)
    picked = jnp.dot(selector, flat, preferred_element_type=jnp.float32).astype(spread.dtype)
    return picked.reshape(spread.shape)


def body(old_tables, table_rows, old_plan, new_plan, ids, bag_len):
    group_count = lax.axis_size("grp")
    col_count = lax.axis_size("col")
    device_count = group_count * col_count
    full_width = old_tables.shape[1]
    table_len = old_tables.shape[2]
    row_block = table_len // device_count
    narrow = full_width // col_count
    per_group = new_plan.shape[0] // group_count
    bag_size = ids.shape[2]
    own_slot = lax.axis_index("grp") * col_count + lax.axis_index("col")
    own_table = old_plan[own_slot]
    row_limit = table_rows[own_table]
    row_iota = lax.broadcasted_iota(jnp.int32, (1, table_len), 1)
    owned_table = old_tables[0] * (row_iota < row_limit).astype(old_tables.dtype)
    spread = lax.all_to_all(
        owned_table.reshape(full_width, device_count, row_block),
        ("grp", "col"),
        split_axis=1,
        concat_axis=0,
        tiled=True,
    )
    spread = spread.reshape(device_count * col_count, narrow, row_block)
    old_inverse = invert(old_plan)
    source_slot = old_inverse[new_plan].reshape(group_count, 1, per_group)
    source_rows = (
        source_slot * col_count + lax.broadcasted_iota(jnp.int32, (1, col_count, 1), 1)
    ).reshape(-1)
    blocks = reorder_blocks(spread, source_rows)
    direct = lax.all_to_all(
        blocks.reshape(device_count, per_group, narrow, row_block),
        ("grp", "col"),
        split_axis=0,
        concat_axis=3,
        tiled=True,
    )
    new_local = direct.reshape(per_group, narrow, table_len)
    bag_iota = lax.broadcasted_iota(jnp.int32, (1, 1, bag_size), 2)
    marked = jnp.where(bag_iota < bag_len[:, :, None], ids, -1)
    by_slot = jnp.take(marked, old_plan, axis=1)
    own_ids = lax.all_to_all(
        by_slot, ("grp", "col"), split_axis=1, concat_axis=0, tiled=True
    ).reshape(-1, bag_size)
    partial_value = pool_rows(owned_table, own_ids)
    returned = lax.all_to_all(
        partial_value.reshape(1, full_width, -1),
        ("grp", "col"),
        split_axis=2,
        concat_axis=0,
        tiled=True,
    )
    by_table = jnp.take(returned, old_inverse, axis=0)
    pooled = jnp.transpose(by_table, (2, 0, 1))
    return (new_local, pooled)


def solution(mesh):
    return jax.shard_map(
        body,
        mesh=mesh,
        in_specs=(
            P(("grp", "col"), None, None),
            P(),
            P(),
            P(),
            P(("grp", "col"), None, None),
            P(("grp", "col"), None),
        ),
        out_specs=(P("grp", "col", None), P(("grp", "col"), None, None)),
        check_vma=False,
    )
```

profile of v0, /device:TPU:9, one launch (start us, length us, event | category | flops | bytes accessed | tf_op | source)
XLA Modules:
  0.0 492.5 jit_solution(5518799861332294195)
XLA Ops:
  0.6 0.7 compare_select_fusion.1
  1.3 0.7 compare_and_fusion
  2.0 0.9 copy.25
  2.9 0.8 copy.24
  3.7 0.1 fusion.1
  3.8 0.6 gather_fusion.1
  4.4 0.1 fusion.5
  4.5 0.7 reshape.168
  5.2 6.3 %all-to-all-start.2 = ((s32[32,1,128]{2,1,0:T(1,128)}), s32[32,1,128]{2,1,0:T(1,128)S(1)}, u32[]{:S(2)}, u32[]{:S(2)}) async-start(s32[32,1,128]{2,1,0:T(1,128)} %reshape.168), calls=%async_computation.2 | async-start | bytes 32768 | tf_op jit(solution)/shard_map/all_to_all | solution.py:75
  11.5 1.2 dynamic_slice.6
  14.7 1.3 dynamic_slice.7
  16.0 0.7 fusion
  16.7 12.4 %copy.28 = bf16[16,8,32,1024]{3,2,1,0:T(8,128)(2,1)} copy(bf16[16,8,32,1024]{3,1,2,0:T(8,128)(2,1)} %bitcast.70) | data formatting | bytes 16777216
  29.1 16.0 %copy_multiply_fusion = bf16[128,32,1024]{2,0,1:T(8,128)(2,1)} fusion(bf16[128,32,1024]{2,1,0:T(8,128)(2,1)} %bitcast.72, bf16[32,1024]{1,0:T(8,128)(2,1)S(1)} %fusion), kind=kLoop, calls=%fused_computation.6 | loop fusion | flops 4194304 | bytes 16842752 | tf_op jit(solution)/shard_map/mul | solution.py:49
  45.1 0.0 all-to-all-done.2
  45.1 5.9 %all-to-all-start = ((bf16[128,32,1024]{2,0,1:T(8,128)(2,1)}), bf16[128,32,1024]{2,0,1:T(8,128)(2,1)}, u32[]{:S(2)}, u32[]{:S(2)}) async-start(bf16[128,32,1024]{2,0,1:T(8,128)(2,1)} %copy_multiply_fusion), calls=%async_computation | async-start | bytes 16777216 | tf_op jit(solution)/shard_map/all_to_all | solution.py:50
  51.0 0.0 copy-start
  51.0 0.0 copy-start.1
  51.0 11.9 %copy.26 = bf16[1,128,32768]{1,2,0:T(8,128)(2,1)} copy(bf16[1,128,32768]{2,1,0:T(8,128)(2,1)} %param.6) | data formatting | bytes 16777216 | tf_op args[0]
  62.9 0.0 copy-done
  62.9 0.0 copy-done.1
  62.9 0.1 select_reduce_fusion
  63.0 0.7 gather_fusion
  63.7 0.1 mul.40
  63.8 0.1 add.73
  64.0 0.7 fusion.2
  64.6 8.6 %bitcast_multiply_fusion = bf16[128,32768]{0,1:T(8,128)(2,1)} fusion(bf16[1,128,32768]{1,2,0:T(8,128)(2,1)} %copy.26, bf16[32768]{0:T(1024)(128)(2,1)S(1)} %fusion.2), kind=kLoop, calls=%fused_computation.5 | loop fusion | flops 4194304 | bytes 16842752 | tf_op jit(solution)/shard_map/mul | solution.py:49
  73.2 0.5 broadcast.144
  73.7 0.7 reduce
  74.4 0.1 reshape.169
  74.5 0.1 reshape.151
  74.6 15.5 %gather_fusion.2 = bf16[4096,128]{1,0:T(8,128)(2,1)S(1)} fusion(bf16[128,32768]{0,1:T(8,128)(2,1)} %bitcast_multiply_fusion, s32[4096]{0:T(1024)S(1)} %broadcast_clamp_fusion), kind=kCustom, calls=%fused_computation.2 | custom fusion | bytes 2113536 | tf_op jit(solution)/shard_map/jit(_take)/gather | solution.py:19
  90.1 2.2 multiply_reduce_fusion
  92.3 144.8 %all-to-all-done = bf16[128,32,1024]{2,0,1:T(8,128)(2,1)} async-done(((bf16[128,32,1024]{2,0,1:T(8,128)(2,1)}), bf16[128,32,1024]{2,0,1:T(8,128)(2,1)}, u32[]{:S(2)}, u32[]{:S(2)}) %all-to-all-start) | async-done | bytes 8388640 | tf_op jit(solution)/shard_map/all_to_all | solution.py:50
  237.1 3.7 all-to-all-start.3
  240.8 13.4 %reshape_reshape.6 = bf16[128,32768]{1,0:T(8,128)(2,1)} reshape(bf16[32,128,1,1024]{3,1,0,2:T(8,128)(2,1)} %bitcast.3) | data formatting | bytes 16777216 | tf_op jit(solution)/shard_map/reshape;reshape | solution.py:30
  254.2 9.0 %convolution_convert_fusion = bf16[128,32768]{1,0:T(8,128)(2,1)} fusion(bf16[128,32768]{1,0:T(8,128)(2,1)} %reshape_reshape.6, s32[128]{0:T(128)S(1)} %add.73), kind=kOutput, calls=%fused_computation.4 | convolution fusion | flops 1077952512 | bytes 16777728 | tf_op jit(solution)/shard_map/dot_general | solution.py:31
  263.2 12.4 %copy.29 = bf16[16,8,32,1024]{3,2,1,0:T(8,128)(2,1)} copy(bf16[16,8,32,1024]{3,1,2,0:T(8,128)(2,1)} %bitcast.69) | data formatting | bytes 16777216
  275.6 0.0 all-to-all-done.3
  275.6 5.9 %all-to-all-start.1 = ((bf16[32,4,32,1024]{3,2,1,0:T(8,128)(2,1)}), bf16[32,4,32,1024]{3,2,1,0:T(8,128)(2,1)}, u32[]{:S(2)}, u32[]{:S(2)}) async-start(bf16[32,4,32,1024]{3,2,1,0:T(8,128)(2,1)} %bitcast.71), calls=%async_computation.1 | async-start | bytes 16777216 | tf_op jit(solution)/shard_map/all_to_all | solution.py:64
  281.6 0.6 gather_fusion.3
  282.2 0.1 select_bitcast_fusion.1
  282.3 0.7 copy.27
  282.9 184.7 %all-to-all-done.1 = bf16[32,4,32,1024]{3,2,1,0:T(8,128)(2,1)} async-done(((bf16[32,4,32,1024]{3,2,1,0:T(8,128)(2,1)}), bf16[32,4,32,1024]{3,2,1,0:T(8,128)(2,1)}, u32[]{:S(2)}, u32[]{:S(2)}) %all-to-all-start.1) | async-done | bytes 8388640 | tf_op jit(solution)/shard_map/all_to_all | solution.py:64
  467.7 11.4 %copy.23 = bf16[1,4,32,32,1024]{4,3,2,1,0:T(8,128)(2,1)} copy(bf16[1,4,32,32,1024]{4,2,1,3,0:T(8,128)(2,1)} %bitcast.5) | data formatting | bytes 16777216 | tf_op jit(solution)/shard_map/all_to_all | solution.py:64
  479.1 13.4 %reshape.129 = bf16[4,32,32768]{2,1,0:T(8,128)(2,1)} reshape(bf16[1,4,32,32,1024]{4,3,2,1,0:T(8,128)(2,1)} %copy.23) | data formatting | bytes 16777216 | tf_op jit(solution)/shard_map/reshape | solution.py:71
  (11 shorter events, 0.1 us)
Async XLA Ops:
  5.2 39.9 %all-to-all-start.2 = ((s32[32,1,128]{2,1,0:T(1,128)}), s32[32,1,128]{2,1,0:T(1,128)S(1)}, u32[]{:S(2)}, u32[]{:S(2)}) async-start(s32[32,1,128]{2,1,0:T(1,128)} %reshape.168), calls=%async_computation.2 | async-start | bytes 32768 | tf_op jit(solution)/shard_map/all_to_all | solution.py:75
  45.1 192.0 %all-to-all-start = ((bf16[128,32,1024]{2,0,1:T(8,128)(2,1)}), bf16[128,32,1024]{2,0,1:T(8,128)(2,1)}, u32[]{:S(2)}, u32[]{:S(2)}) async-start(bf16[128,32,1024]{2,0,1:T(8,128)(2,1)} %copy_multiply_fusion), calls=%async_computation | async-start | bytes 16777216 | tf_op jit(solution)/shard_map/all_to_all | solution.py:50
  51.0 11.9 %copy-start = (s32[32]{0:T(128)S(1)}, s32[32]{0:T(128)}, u32[]{:S(2)}) copy-start(s32[32]{0:T(128)} %param.9) | copy-start | bytes 388
  51.0 11.9 %copy-start.1 = (s32[32]{0:T(128)S(1)}, s32[32]{0:T(128)}, u32[]{:S(2)}) copy-start(s32[32]{0:T(128)} %param.8) | copy-start | bytes 388
  237.1 38.5 %all-to-all-start.3 = ((f32[1,128,256]{1,0,2:T(1,128)}), f32[1,128,256]{1,0,2:T(1,128)S(1)}, u32[]{:S(2)}, u32[]{:S(2)}) async-start(f32[1,128,256]{1,0,2:T(1,128)} %bitcast.18), calls=%async_computation.3 | async-start | bytes 262144 | tf_op jit(solution)/shard_map/all_to_all | solution.py:79
  275.6 192.0 %all-to-all-start.1 = ((bf16[32,4,32,1024]{3,2,1,0:T(8,128)(2,1)}), bf16[32,4,32,1024]{3,2,1,0:T(8,128)(2,1)}, u32[]{:S(2)}, u32[]{:S(2)}) async-start(bf16[32,4,32,1024]{3,2,1,0:T(8,128)(2,1)} %bitcast.71), calls=%async_computation.1 | async-start | bytes 16777216 | tf_op jit(solution)/shard_map/all_to_all | solution.py:64
where the time goes:
time: 494 us; the launch traced here: 492 us
  waiting for transfers between devices  329 us (67%)
  local copies, waits for them, and re-layouts  98.9 us (20%)
  other arithmetic  30.6 us (6%)
  starting transfers between devices  21.8 us (4%)
  matrix products  8.98 us (2%)
    all_to_all x1, waiting for transfers between devices, body(): lax.all_to_all(blocks.reshape(device_count, per_group, narrow, row_block)...  185 us
    all_to_all x1, waiting for transfers between devices, body(): lax.all_to_all(owned_table.reshape(full_width, device_count, row_block),...  145 us
    unnamed x12, local copies, waits for them, and re-layouts  39.9 us
    mul x2, other arithmetic, body(): old_tables[0] * (row_iota < row_limit).astype(old_tables.dtype)  24.6 us
    gather x1, local copies, waits for them, and re-layouts, pool_rows(): jnp.take(table_cols, safe_ids, axis=1)  15.5 us
    another operation x1, local copies, waits for them, and re-layouts, reorder_blocks(): flat = spread.reshape(count, -1)  13.4 us
    reshape x1, local copies, waits for them, and re-layouts, body(): new_local = direct.reshape(per_group, narrow, table_len)  13.4 us
    all_to_all x1, local copies, waits for them, and re-layouts, body(): lax.all_to_all(blocks.reshape(device_count, per_group, narrow, row_block)...  11.4 us
  transfers between devices with their start and end apart: 4, of which 2 were waited for; matrix products, arithmetic and copies ran while one was open for 22% of the time, Pallas kernels for 0%

commit v1 on v0

--- a/solution.py
+++ b/solution.py
@@ -2,6 +2,13 @@
 import jax.numpy as jnp
 from jax import lax
 from jax.sharding import PartitionSpec as P
+
+
+def stacked_exchange(block, axis, split, join):
+    n_dev = lax.axis_size(axis)
+    blocks = jnp.stack(jnp.split(block, n_dev, axis=split), axis=0)
+    blocks = lax.all_to_all(blocks, axis, split_axis=0, concat_axis=0)
+    return jnp.concatenate(blocks, axis=join)
 
 
 def invert(permutation):
@@ -47,12 +54,8 @@
     row_limit = table_rows[own_table]
     row_iota = lax.broadcasted_iota(jnp.int32, (1, table_len), 1)
     owned_table = old_tables[0] * (row_iota < row_limit).astype(old_tables.dtype)
-    spread = lax.all_to_all(
-        owned_table.reshape(full_width, device_count, row_block),
-        ("grp", "col"),
-        split_axis=1,
-        concat_axis=0,
-        tiled=True,
+    spread = stacked_exchange(
+        owned_table.reshape(full_width, device_count, row_block), ("grp", "col"), 1, 0
     )
     spread = spread.reshape(device_count * col_count, narrow, row_block)
     old_inverse = invert(old_plan)

time: 494 us -> 520 us (1.053)
  local copies, waits for them, and re-layouts: 98.9 us -> 121 us
  waiting for transfers between devices: 329 us -> 341 us
  other arithmetic: 30.6 us -> 21.6 us
    all_to_all x1, waiting for transfers between devices: 145 us -> 157 us  [stacked_exchange(): blocks = lax.all_to_all(blocks, axis, split_axis=0, concat_axis=0)]
    all_to_all x0 -> x1, local copies, waits for them, and re-layouts: none -> 11.9 us  [stacked_exchange(): blocks = lax.all_to_all(blocks, axis, split_axis=0, concat_axis=0)]
    unnamed x12 -> x40, local copies, waits for them, and re-layouts: 39.9 us -> 49.8 us
    mul x2, other arithmetic: 24.6 us -> 14.9 us  [body(): old_tables[0] * (row_iota < row_limit).astype(old_tables.dtype)]
  transfers between devices with their start and end apart: 4 -> 4, of which waited for: 2 -> 2; matrix products, arithmetic and copies ran while one was open for 22% -> 24% of each run, Pallas kernels for 0% -> 0%
where the time goes in v1:
time: 520 us; the launch traced here: 518 us
  waiting for transfers between devices  341 us (66%)
  local copies, waits for them, and re-layouts  121 us (23%)
  starting transfers between devices  21.8 us (4%)
  other arithmetic  21.6 us (4%)
  matrix products  9.15 us (2%)
    all_to_all x1, waiting for transfers between devices, body(): lax.all_to_all(blocks.reshape(device_count, per_group, narrow, row_block)...  185 us
    all_to_all x1, waiting for transfers between devices, stacked_exchange(): blocks = lax.all_to_all(blocks, axis, split_axis=0, concat_axis=0)  157 us
    unnamed x40, local copies, waits for them, and re-layouts  49.8 us
    gather x1, local copies, waits for them, and re-layouts, pool_rows(): jnp.take(table_cols, safe_ids, axis=1)  15.5 us
    mul x2, other arithmetic, body(): old_tables[0] * (row_iota < row_limit).astype(old_tables.dtype)  14.9 us
    another operation x1, local copies, waits for them, and re-layouts, reorder_blocks(): flat = spread.reshape(count, -1)  13.5 us
    reshape x1, local copies, waits for them, and re-layouts, body(): new_local = direct.reshape(per_group, narrow, table_len)  13.4 us
    all_to_all x1, local copies, waits for them, and re-layouts, stacked_exchange(): blocks = lax.all_to_all(blocks, axis, split_axis=0, concat_axis=0)  11.9 us
  transfers between devices with their start and end apart: 4, of which 2 were waited for; matrix products, arithmetic and copies ran while one was open for 24% of the time, Pallas kernels for 0%

profile of v1, /device:TPU:9, one launch (start us, length us, event | category | flops | bytes accessed | tf_op | source)
XLA Modules:
  0.0 518.2 jit_solution(194304524486270480)
XLA Ops:
  2.6 0.8 copy.77
  3.4 0.9 copy.78
  5.1 0.7 reshape.167
  5.9 6.3 %all-to-all-start.2 = ((s32[32,1,128]{2,1,0:T(1,128)}), s32[32,1,128]{2,1,0:T(1,128)S(1)}, u32[]{:S(2)}, u32[]{:S(2)}) async-start(s32[32,1,128]{2,1,0:T(1,128)} %reshape.167), calls=%async_computation.2 | async-start | bytes 32768 | tf_op jit(solution)/shard_map/all_to_all | solution.py:78
  12.2 1.2 dynamic_slice.6
  15.4 1.3 dynamic_slice.7
  17.3 11.9 %copy.72 = bf16[1,128,32768]{1,2,0:T(8,128)(2,1)} copy(bf16[1,128,32768]{2,1,0:T(8,128)(2,1)} %param.6) | data formatting | bytes 16777216 | tf_op args[0]
  29.2 6.4 %broadcast_multiply_fusion = bf16[128,32,1024]{0,2,1:T(8,128)(2,1)S(1)} fusion(bf16[128,32,1024]{0,2,1:T(8,128)(2,1)} %bitcast.191, bf16[32,1024]{1,0:T(8,128)(2,1)S(1)} %fusion.32), kind=kLoop, calls=%fused_computation.6 | loop fusion | flops 4194304 | bytes 16842752 | tf_op jit(solution)/shard_map/mul | solution.py:56
  35.6 0.7 fusion.31
  36.3 0.7 fusion.30
  37.1 0.7 fusion.29
  37.8 0.7 fusion.28
  39.3 0.7 fusion.26
  40.0 0.7 fusion.25
  41.4 0.7 fusion.23
  42.2 0.7 fusion.22
  42.9 0.7 fusion.21
  45.0 0.7 fusion.18
  45.8 0.7 fusion.17
  47.2 0.7 fusion.15
  47.9 0.7 fusion.14
  48.7 0.7 fusion.13
  49.4 0.7 fusion.12
  50.1 0.7 fusion.11
  50.8 0.7 fusion.10
  52.3 0.7 fusion.8
  53.0 0.7 fusion.7
  53.7 0.7 fusion.6
  54.4 0.7 fusion.5
  55.2 0.7 fusion.4
  55.9 0.7 fusion.3
  56.6 0.7 fusion.2
  57.3 0.7 fusion.1
  58.1 0.7 fusion
  58.8 5.9 %all-to-all-start = ((bf16[32,128,1,1024]{1,3,2,0:T(8,128)(2,1)}), bf16[32,128,1,1024]{1,3,2,0:T(8,128)(2,1)}, u32[]{:S(2)}, u32[]{:S(2)}) async-start(bf16[32,128,1,1024]{1,3,2,0:T(8,128)(2,1)} %fusion), calls=%async_computation | async-start | bytes 16777216 | tf_op jit(solution)/shard_map/all_to_all | solution.py:10
  66.4 8.6 %bitcast_multiply_fusion = bf16[128,32768]{0,1:T(8,128)(2,1)} fusion(bf16[1,128,32768]{1,2,0:T(8,128)(2,1)} %copy.72, bf16[32768]{0:T(1024)(128)(2,1)S(1)} %fusion.34), kind=kLoop, calls=%fused_computation.5 | loop fusion | flops 4194304 | bytes 16842752 | tf_op jit(solution)/shard_map/mul | solution.py:56
  76.4 15.5 %gather_fusion.2 = bf16[4096,128]{1,0:T(8,128)(2,1)S(1)} fusion(bf16[128,32768]{0,1:T(8,128)(2,1)} %bitcast_multiply_fusion, s32[4096]{0:T(1024)S(1)} %broadcast_clamp_fusion), kind=kCustom, calls=%fused_computation.2 | custom fusion | bytes 2113536 | tf_op jit(solution)/shard_map/jit(_take)/gather | solution.py:26
  92.0 2.2 multiply_reduce_fusion
  94.1 156.7 %all-to-all-done = bf16[32,128,1,1024]{1,3,2,0:T(8,128)(2,1)} async-done(((bf16[32,128,1,1024]{1,3,2,0:T(8,128)(2,1)}), bf16[32,128,1,1024]{1,3,2,0:T(8,128)(2,1)}, u32[]{:S(2)}, u32[]{:S(2)}) %all-to-all-start) | async-done | bytes 8388640 | tf_op jit(solution)/shard_map/all_to_all | solution.py:10
  250.9 3.7 all-to-all-start.3
  254.6 11.9 %copy.75 = bf16[32,128,1,1024]{3,1,0,2:T(8,128)(2,1)} copy(bf16[32,128,1,1024]{1,3,2,0:T(8,128)(2,1)} %all-to-all-done) | data formatting | bytes 16777216 | tf_op jit(solution)/shard_map/all_to_all | solution.py:10
  266.5 13.5 %reshape_reshape_reshape.3 = bf16[128,32768]{1,0:T(8,128)(2,1)} reshape(bf16[32,128,1,1024]{3,1,0,2:T(8,128)(2,1)} %copy.75) | data formatting | bytes 16777216 | tf_op jit(solution)/shard_map/reshape;reshape;reshape | solution.py:37
  280.0 9.2 %convolution_convert_fusion = bf16[128,32768]{1,0:T(8,128)(2,1)} fusion(bf16[128,32768]{1,0:T(8,128)(2,1)} %reshape_reshape_reshape.3, s32[128]{0:T(128)S(1)} %add.73), kind=kOutput, calls=%fused_computation.4 | convolution fusion | flops 1077952512 | bytes 16777728 | tf_op jit(solution)/shard_map/dot_general | solution.py:38
  289.1 12.2 %copy.82 = bf16[16,8,32,1024]{3,2,1,0:T(8,128)(2,1)} copy(bf16[16,8,32,1024]{3,1,2,0:T(8,128)(2,1)} %bitcast.193) | data formatting | bytes 16777216
  301.4 5.9 %all-to-all-start.1 = ((bf16[32,4,32,1024]{3,2,1,0:T(8,128)(2,1)}), bf16[32,4,32,1024]{3,2,1,0:T(8,128)(2,1)}, u32[]{:S(2)}, u32[]{:S(2)}) async-start(bf16[32,4,32,1024]{3,2,1,0:T(8,128)(2,1)} %bitcast.194), calls=%async_computation.1 | async-start | bytes 16777216 | tf_op jit(solution)/shard_map/all_to_all | solution.py:67
  308.7 184.7 %all-to-all-done.1 = bf16[32,4,32,1024]{3,2,1,0:T(8,128)(2,1)} async-done(((bf16[32,4,32,1024]{3,2,1,0:T(8,128)(2,1)}), bf16[32,4,32,1024]{3,2,1,0:T(8,128)(2,1)}, u32[]{:S(2)}, u32[]{:S(2)}) %all-to-all-start.1) | async-done | bytes 8388640 | tf_op jit(solution)/shard_map/all_to_all | solution.py:67
  493.4 11.4 %copy.76 = bf16[1,4,32,32,1024]{4,3,2,1,0:T(8,128)(2,1)} copy(bf16[1,4,32,32,1024]{4,2,1,3,0:T(8,128)(2,1)} %bitcast.36) | data formatting | bytes 16777216 | tf_op jit(solution)/shard_map/all_to_all | solution.py:67
  504.8 13.4 %reshape.128 = bf16[4,32,32768]{2,1,0:T(8,128)(2,1)} reshape(bf16[1,4,32,32,1024]{4,3,2,1,0:T(8,128)(2,1)} %copy.76) | data formatting | bytes 16777216 | tf_op jit(solution)/shard_map/reshape | solution.py:74
  (38 shorter events, 12.2 us)
Async XLA Ops:
  5.9 53.0 %all-to-all-start.2 = ((s32[32,1,128]{2,1,0:T(1,128)}), s32[32,1,128]{2,1,0:T(1,128)S(1)}, u32[]{:S(2)}, u32[]{:S(2)}) async-start(s32[32,1,128]{2,1,0:T(1,128)} %reshape.167), calls=%async_computation.2 | async-start | bytes 32768 | tf_op jit(solution)/shard_map/all_to_all | solution.py:78
  58.8 5.9 %copy-start = (s32[32]{0:T(128)S(1)}, s32[32]{0:T(128)}, u32[]{:S(2)}) copy-start(s32[32]{0:T(128)} %param.8) | copy-start | bytes 388
  58.8 192.0 %all-to-all-start = ((bf16[32,128,1,1024]{1,3,2,0:T(8,128)(2,1)}), bf16[32,128,1,1024]{1,3,2,0:T(8,128)(2,1)}, u32[]{:S(2)}, u32[]{:S(2)}) async-start(bf16[32,128,1,1024]{1,3,2,0:T(8,128)(2,1)} %fusion), calls=%async_computation | async-start | bytes 16777216 | tf_op jit(solution)/shard_map/all_to_all | solution.py:10
  250.9 50.5 %all-to-all-start.3 = ((f32[1,128,256]{1,0,2:T(1,128)}), f32[1,128,256]{1,0,2:T(1,128)S(1)}, u32[]{:S(2)}, u32[]{:S(2)}) async-start(f32[1,128,256]{1,0,2:T(1,128)} %bitcast.49), calls=%async_computation.3 | async-start | bytes 262144 | tf_op jit(solution)/shard_map/all_to_all | solution.py:82
  301.4 192.0 %all-to-all-start.1 = ((bf16[32,4,32,1024]{3,2,1,0:T(8,128)(2,1)}), bf16[32,4,32,1024]{3,2,1,0:T(8,128)(2,1)}, u32[]{:S(2)}, u32[]{:S(2)}) async-start(bf16[32,4,32,1024]{3,2,1,0:T(8,128)(2,1)} %bitcast.194), calls=%async_computation.1 | async-start | bytes 16777216 | tf_op jit(solution)/shard_map/all_to_all | solution.py:67
